TPU v7x, 32 devices: a whole 2x2x4 slice. The times are simulated.
32 devices in a mesh: blk: 8 (over y, x, core), grp: 4 (over z).
Axes of the slice: x: 2, y: 2, z: 4, core: 2. Of those that a mesh axis runs over, the one named last changes fastest.
Arguments:
- queries: bfloat16 [48, 8192], P(None, ('blk', 'grp')), may hold values from -6 to 6
- key_pool: bfloat16 [4, 64, 128, 1024], P('grp', 'blk'), may hold values from -28 to 28
- value_pool: bfloat16 [4, 64, 128, 1024], P('grp', 'blk'), may hold values from -6 to 6
- lengths: int32 [4, 4], P('grp'), may hold values from 1 to 32, as said below
- block_table: int32 [4, 4, 32], P('grp'), may hold values from 0 to 63, as said below
Outputs:
- attended: bfloat16 [48, 8192], P('grp', 'blk')
Inputs may be any that keep to these rules, and one draw needn't show every extreme that they name: Each group's 4 lengths add up to 52, and one of them is exactly 32. Within a group, the entries block_table[g, q, j] with j < lengths[g, q] are distinct slots; entries past a sequence's length are arbitrary slots and unused. Slots s * 8 to s * 8 + 7 form the s-th aligned block of the pool; at least 4 and at most 8 live slots lie in one aligned block, and exactly 8 in some aligned block of every group.
All inputs are finite; a program needn't handle non-finite values.
Results may differ from a plain program's by a relative error of at most 0.0049.
Values may be sent and summed in bfloat16 or wider, within the bound.
A program may use at most 64 MiB of HBM per device.

v0:
```python
import functools
import math

import jax
import jax.numpy as jnp
from jax import lax
from jax.experimental import pallas as pl
from jax.experimental.pallas import tpu as pltpu
from jax.sharding import PartitionSpec as P

HQ = 64
KVH = 8
DH = 128
STEPS = 3


empty_max = -1e30


def owners(seq_lengths, slot_table, first_slot, slot_count):
    slot_ids = first_slot + jnp.arange(slot_count, dtype=jnp.int32)
    places = jnp.arange(slot_table.shape[1], dtype=jnp.int32)
    in_length = places[None, :] < seq_lengths[:, None]
    matches = (slot_table[:, :, None] == slot_ids[None, None, :]) & in_length[:, :, None]
    return jnp.transpose(jnp.any(matches, axis=1))


def slot_partials(query_block, key_block, value_block):
    slot_count = key_block.shape[0]
    per_group = HQ // KVH
    grouped_q = query_block.reshape(slot_count, STEPS, KVH, per_group, DH)
    grouped_q = jnp.transpose(grouped_q, (0, 2, 1, 3, 4)).reshape(
        slot_count, KVH, STEPS * per_group, DH
    )
    key_heads = key_block.reshape(slot_count, key_block.shape[1], KVH, DH)
    value_heads = value_block.reshape(slot_count, value_block.shape[1], KVH, DH)
    scores = jnp.einsum(
        "cgqd,ctgd->cgqt", grouped_q, key_heads, preferred_element_type=jnp.float32
    ) * (1.0 / math.sqrt(DH))
    block_max = jnp.max(scores, axis=3)
    weights = jnp.exp(scores - block_max[..., None]).astype(jnp.bfloat16)
    block_total = jnp.sum(weights.astype(jnp.float32), axis=3)
    block_out = jnp.einsum(
        "cgqt,ctgd->cgqd", weights, value_heads, preferred_element_type=jnp.float32
    )
    return (block_max, block_total, block_out)


def gather_sequences(owned, block_max, block_total, block_out):
    masked = jnp.where(owned[:, :, None, None], block_max[:, None], empty_max)
    seq_max = jnp.max(masked, axis=0)
    factor = jnp.where(owned[:, :, None, None], jnp.exp(block_max[:, None] - seq_max[None]), 0.0)
    seq_total = jnp.sum(factor * block_total[:, None], axis=0)
    seq_out = jnp.einsum("cqgh,cghd->qghd", factor, block_out, precision=lax.Precision.HIGHEST)
    seq_count = owned.shape[1]
    per_group = HQ // KVH
    seq_max = jnp.transpose(
        seq_max.reshape(seq_count, KVH, STEPS, per_group), (0, 2, 1, 3)
    ).reshape(seq_count * STEPS, HQ)
    seq_total = jnp.transpose(
        seq_total.reshape(seq_count, KVH, STEPS, per_group), (0, 2, 1, 3)
    ).reshape(seq_count * STEPS, HQ)
    seq_out = jnp.transpose(
        seq_out.reshape(seq_count, KVH, STEPS, per_group, DH), (0, 2, 1, 3, 4)
    ).reshape(seq_count * STEPS, HQ, DH)
    return (seq_max, seq_total, seq_out)


def block_summary(owned, query_seq, key_block, value_block):
    query_block = jnp.dot(
        owned.astype(jnp.bfloat16), query_seq, preferred_element_type=jnp.float32
    ).astype(jnp.bfloat16)
    block_max, block_total, block_out = slot_partials(query_block, key_block, value_block)
    return gather_sequences(owned, block_max, block_total, block_out)


def body(queries, key_pool, value_pool, lengths, block_table):
    grouped = lax.all_to_all(queries, "grp", split_axis=0, concat_axis=1, tiled=True)
    query_full = lax.all_gather(grouped, "blk", axis=1, tiled=True)
    token_count = query_full.shape[0]
    query_seq = query_full.reshape(token_count // STEPS, STEPS * query_full.shape[1])
    local_keys = key_pool[0]
    local_values = value_pool[0]
    slots_here = local_keys.shape[0]
    first_slot = lax.axis_index("blk") * slots_here
    owned = owners(lengths[0], block_table[0], first_slot, slots_here)
    seq_max, seq_total, seq_out = block_summary(owned, query_seq, local_keys, local_values)
    cycle_size = lax.axis_size("blk")
    heads_here = HQ // cycle_size
    arrived_max, arrived_total, arrived_out = (
        lax.all_to_all(seq_max[None], "blk", split_axis=2, concat_axis=0, tiled=True),
        lax.all_to_all(seq_total[None], "blk", split_axis=2, concat_axis=0, tiled=True),
        lax.all_to_all(seq_out[None], "blk", split_axis=2, concat_axis=0, tiled=True),
    )
    slice_max = jnp.max(arrived_max, axis=0)
    scaling = jnp.exp(arrived_max - slice_max[None])
    mine_total = jnp.sum(scaling * arrived_total, axis=0)
    mine_out = jnp.sum(scaling[..., None] * arrived_out, axis=0)
    attended = (mine_out / mine_total[..., None]).astype(jnp.bfloat16)
    return attended.reshape(mine_out.shape[0], heads_here * DH)


LANES = 128
SUB = 8


def flip(index, step):
    bit = 1
    while bit <= step:
        if step & bit:
            index = index + bit * (1 - 2 * ((index // bit) % 2))
        bit *= 2
    return index


def runs_of(tokens, heads):
    out = []
    for block in range(tokens * heads // SUB):
        row = 0
        while row < SUB:
            head, token = divmod(block * SUB + row, tokens)
            count = min(SUB - row, tokens - token)
            out.append((block, row, head, token, count))
            row += count
    return out


def fused(
    n_blk, n_grp, seqs, tokens, heads, per_group,
    q_hbm, k_hbm, v_hbm, len_hbm, table_hbm, out_ref,
    q_in, q_f32, q_send, q_buf, k_buf, v_buf, q_rows, o_send, o_recv, s_send, s_recv, o_rows,
    table_ref, len_ref, owner_ref, in_sem, kv_sem, z_send, z_recv, p_send, p_recv, o_ssem, o_rsem, s_ssem, s_rsem,
):
    b = lax.axis_index("blk")
    g = lax.axis_index("grp")
    slots = k_hbm.shape[1]
    runs = runs_of(tokens, heads)
    rows_seq = STEPS * per_group
    rows = seqs * rows_seq
    scale = math.log2(math.e) / math.sqrt(DH)

    barrier = pltpu.get_barrier_semaphore()
    for d in range(1, n_grp):
        pl.semaphore_signal(barrier, inc=1, device_id={"grp": flip(g, d)}, device_id_type=pl.DeviceIdType.MESH)
    for r in range(1, n_blk):
        pl.semaphore_signal(barrier, inc=1, device_id={"blk": flip(b, r)}, device_id_type=pl.DeviceIdType.MESH)

    q_copy = pltpu.make_async_copy(q_hbm, q_in, in_sem.at[0])
    table_copy = pltpu.make_async_copy(table_hbm, table_ref, in_sem.at[1])
    len_copy = pltpu.make_async_copy(len_hbm, len_ref, in_sem.at[2])
    q_copy.start()
    table_copy.start()
    len_copy.start()
    kv_copies = []
    for s in range(slots):
        kv_copies.append(pltpu.make_async_copy(k_hbm.at[0, s], k_buf.at[s], kv_sem.at[0, s]))
        kv_copies.append(pltpu.make_async_copy(v_hbm.at[0, s], v_buf.at[s], kv_sem.at[1, s]))
    for copy in kv_copies:
        copy.start()

    q_copy.wait()
    q_f32[...] = q_in[...].astype(jnp.float32)

    def pack(group, store):
        for block in range(tokens * heads // SUB):
            parts = [
                q_f32[group * tokens + t0 : group * tokens + t0 + count, hh * DH : (hh + 1) * DH]
                for (blk_i, _, hh, t0, count) in runs
                if blk_i == block
            ]
            piece = parts[0] if len(parts) == 1 else jnp.concatenate(parts, axis=0)
            store(block, piece.astype(jnp.bfloat16))

    for group in range(n_grp):
        def put(block, piece, group=group):
            q_send[group, block] = piece
        pack(group, put)
    q_buf[0, g] = q_send[g]

    table_copy.wait()
    len_copy.wait()
    table = table_ref[0]
    seq_id = lax.broadcasted_iota(jnp.int32, table.shape, 0)
    place = lax.broadcasted_iota(jnp.int32, table.shape, 1)
    length = jnp.zeros(table.shape, jnp.int32)
    for q in range(seqs):
        length = jnp.where(seq_id == q, jnp.broadcast_to(len_ref[0:1, q : q + 1], table.shape), length)
    o_masks = []
    marked = jnp.where(place < length, table - b * slots, -1)
    for s in range(slots):
        owner = jnp.max(jnp.where(marked == s, seq_id, -1), axis=1, keepdims=True)
        owner = jnp.max(owner, axis=0, keepdims=True)
        o_masks.append(jnp.broadcast_to(owner, (SUB, LANES)))
    owner_ref[...] = jnp.stack(o_masks)

    pl.semaphore_wait(barrier, n_grp - 1 + n_blk - 1)

    def z_copy(d):
        there = flip(g, d)
        return pltpu.make_async_remote_copy(
            src_ref=q_send.at[there], dst_ref=q_buf.at[0, g],
            send_sem=z_send.at[d], recv_sem=z_recv.at[d],
            device_id={"grp": there}, device_id_type=pl.DeviceIdType.MESH,
        )

    def forward(group):
        for r in range(n_blk - 1, 0, -1):
            pltpu.make_async_remote_copy(
                src_ref=q_buf.at[0, group], dst_ref=q_buf.at[r, group],
                send_sem=p_send.at[r], recv_sem=p_recv.at[r],
                device_id={"blk": flip(b, r)}, device_id_type=pl.DeviceIdType.MESH,
            ).start()

    def whole(r):
        return pltpu.make_async_remote_copy(
            src_ref=q_buf.at[0], dst_ref=q_buf.at[r],
            send_sem=p_send.at[r], recv_sem=p_recv.at[r],
            device_id={"blk": flip(b, r)}, device_id_type=pl.DeviceIdType.MESH,
        )

    order = range(1, n_grp)
    z_copies = {d: z_copy(d) for d in order}
    for d in reversed(order):
        z_copies[d].start()
    forward(g)
    for d in order:
        z_copies[d].wait_recv()
        forward(flip(g, d))

    for copy in kv_copies:
        copy.wait()

    def head(r):
        k = flip(b, r)
        lanes = pl.ds(pl.multiple_of(k * DH, DH), DH)
        rows_ref = q_rows.at[r % 2]
        for piece in range(n_grp):
            values = q_buf[r, piece].astype(jnp.float32)
            for block, row, hh, t0, count in runs:
                rows_ref[pl.ds(t0 * per_group + piece * heads + hh, count, stride=per_group), :] = values[
                    block, row : row + count
                ]
        seq_rows = [rows_ref[q * rows_seq : (q + 1) * rows_seq] for q in range(seqs)]
        scores, owned = [], []
        for s in range(slots):
            owner = jnp.concatenate([owner_ref[s]] * (rows_seq // SUB), axis=0)
            owned.append([owner == q for q in range(seqs)])
            mine = seq_rows[0]
            for q in range(1, seqs):
                mine = jnp.where(owned[s][q], seq_rows[q], mine)
            scores.append(
                lax.dot_general(
                    mine.astype(jnp.bfloat16), k_buf[s, :, lanes],
                    (((1,), (1,)), ((), ())), preferred_element_type=jnp.float32,
                )
            )
        tops = []
        for q in range(seqs):
            top = jnp.full((rows_seq, LANES), empty_max, jnp.float32)
            for s in range(slots):
                top = jnp.where(owned[s][q], jnp.maximum(top, scores[s]), top)
            tops.append(jnp.broadcast_to(jnp.max(top, axis=1, keepdims=True) * scale, (rows_seq, LANES)))
        weights = []
        for s in range(slots):
            top = tops[0]
            for q in range(1, seqs):
                top = jnp.where(owned[s][q], tops[q], top)
            weight = jnp.exp2(scores[s] * scale - top)
            weights.append(
                jnp.concatenate(
                    [jnp.where(owned[s][q], weight, 0.0) for q in range(seqs)], axis=0
                ).astype(jnp.bfloat16)
            )
        weights = jnp.concatenate(weights, axis=1)
        values = v_buf[:, :, lanes].reshape(slots * v_buf.shape[1], DH)
        values = jnp.concatenate([values, jnp.ones((values.shape[0], LANES), jnp.bfloat16)], axis=1)
        total = jnp.dot(weights, values, preferred_element_type=jnp.float32)
        return total[:, :DH].astype(jnp.bfloat16), (tops, total[:, DH:])

    def in_rows(tops, total):
        lane = lax.broadcasted_iota(jnp.int32, (rows, LANES), 1)
        stats = jnp.where(lane == 0, jnp.concatenate(tops, axis=0), total)
        stats = jnp.concatenate([stats, jnp.zeros((LANES - rows, LANES), jnp.float32)], axis=0)
        return jnp.transpose(stats)[:SUB]

    def o_copy(r):
        return pltpu.make_async_remote_copy(
            src_ref=o_send.at[r], dst_ref=o_recv.at[r],
            send_sem=o_ssem.at[r], recv_sem=o_rsem.at[r],
            device_id={"blk": flip(b, r)}, device_id_type=pl.DeviceIdType.MESH,
        )

    def s_copy(r):
        return pltpu.make_async_remote_copy(
            src_ref=s_send.at[r], dst_ref=s_recv.at[r],
            send_sem=s_ssem.at[r], recv_sem=s_rsem.at[r],
            device_id={"blk": flip(b, r)}, device_id_type=pl.DeviceIdType.MESH,
        )

    for pair in [(r, r + 1) for r in range(0, n_blk - 2, 2)] + [(n_blk - 2,), (n_blk - 1,)]:
        for r in pair:
            if r:
                whole(r).wait_recv()
        results = [head(r) for r in pair]
        for r, (o, _) in zip(pair, results):
            if r:
                o_send[r] = o
                o_copy(r).start()
            else:
                o_recv[0] = o
        for r, (_, stats) in zip(pair, results):
            if r:
                s_send[r] = in_rows(*stats)
                s_copy(r).start()
            else:
                s_recv[0] = in_rows(*stats)

    for r in range(1, n_blk):
        s_copy(r).wait_recv()
    tops = s_recv[:, 0, :]
    factor = jnp.exp2(tops - jnp.max(tops, axis=0, keepdims=True))
    share = factor / jnp.sum(factor * s_recv[:, 1, :], axis=0, keepdims=True)
    share = jnp.concatenate([share, jnp.zeros((LANES - n_blk, LANES), jnp.float32)], axis=0)
    share = jnp.transpose(share)[:rows]
    merged = jnp.zeros((rows, DH), jnp.float32)
    for r in range(n_blk):
        if r:
            o_copy(r).wait_recv()
        merged = merged + share[:, r : r + 1] * o_recv[r].astype(jnp.float32)
    o_rows[...] = merged
    for h in range(per_group):
        out_ref[:, h * DH : (h + 1) * DH] = o_rows[pl.ds(h, tokens, stride=per_group), :].astype(jnp.bfloat16)

    for d in order:
        z_copies[d].wait_send()
    for r in range(1, n_blk):
        whole(r).wait_send()
        o_copy(r).wait_send()
        s_copy(r).wait_send()


def fused_body(n_blk, n_grp, queries, key_pool, value_pool, lengths, block_table):
    seqs = lengths.shape[1]
    tokens = seqs * STEPS
    heads = queries.shape[1] // DH
    per_group = HQ // KVH
    slots, block = key_pool.shape[1:3]
    rows = tokens * per_group
    blocks = tokens * heads // SUB
    dma = pltpu.SemaphoreType.DMA
    vmem = pl.BlockSpec(memory_space=pltpu.VMEM)
    hbm = pl.BlockSpec(memory_space=pltpu.HBM)
    return pl.pallas_call(
        functools.partial(fused, n_blk, n_grp, seqs, tokens, heads, per_group),
        out_shape=pltpu.VMEM((tokens, per_group * DH), jnp.bfloat16),
        in_specs=[hbm] * 5,
        out_specs=vmem,
        scratch_shapes=[
            pltpu.VMEM(queries.shape, jnp.bfloat16),
            pltpu.VMEM(queries.shape, jnp.float32),
            pltpu.VMEM((n_grp, blocks, SUB, DH), jnp.bfloat16),
            pltpu.VMEM((n_blk, n_grp, blocks, SUB, DH), jnp.bfloat16),
            pltpu.VMEM((slots, block, KVH * DH), jnp.bfloat16),
            pltpu.VMEM((slots, block, KVH * DH), jnp.bfloat16),
            pltpu.VMEM((2, rows, DH), jnp.float32),
            pltpu.VMEM((n_blk, rows, DH), jnp.bfloat16),
            pltpu.VMEM((n_blk, rows, DH), jnp.bfloat16),
            pltpu.VMEM((n_blk, SUB, LANES), jnp.float32),
            pltpu.VMEM((n_blk, SUB, LANES), jnp.float32),
            pltpu.VMEM((rows, DH), jnp.float32),
            pltpu.VMEM(block_table.shape, jnp.int32),
            pltpu.VMEM(lengths.shape, jnp.int32),
            pltpu.VMEM((slots, SUB, LANES), jnp.int32),
            dma((3,)), dma((2, slots)),
            dma((n_grp,)), dma((n_grp,)),
            dma((n_blk,)), dma((n_blk,)),
            dma((n_blk,)), dma((n_blk,)),
            dma((n_blk,)), dma((n_blk,)),
        ],
        compiler_params=pltpu.CompilerParams(
            collective_id=0, has_side_effects=True, vmem_limit_bytes=62914560
        ),
    )(queries, key_pool, value_pool, lengths, block_table)


def choose(mesh):
    n_blk, n_grp = mesh.shape["blk"], mesh.shape["grp"]

    def run(queries, key_pool, value_pool, lengths, block_table):
        rows = lengths.shape[1] * HQ // KVH * STEPS
        fits = (
            n_blk == KVH
            and n_blk & (n_blk - 1) == 0
            and n_grp & (n_grp - 1) == 0
            and queries.shape[1] % DH == 0
            and (lengths.shape[1] * STEPS * queries.shape[1] // DH) % SUB == 0
            and rows % 16 == 0
            and rows <= LANES
            and key_pool.shape[2] == LANES
        )
        if not fits:
            return body(queries, key_pool, value_pool, lengths, block_table)
        return fused_body(n_blk, n_grp, queries, key_pool, value_pool, lengths, block_table)

    return run


def solution(mesh):
    placed = (
        P(None, ("blk", "grp")),
        P("grp", "blk", None, None),
        P("grp", "blk", None, None),
        P("grp", None),
        P("grp", None, None),
    )
    return jax.shard_map(
        choose(mesh), mesh=mesh, in_specs=placed, out_specs=P("grp", "blk"), check_vma=False
    )
```

profile of v0, /device:TPU:0, one launch (start us, length us, event | category | flops | bytes accessed | tf_op | source)
XLA Modules:
  0.0 20.8 jit_solution(14831617618226223117)
XLA Ops:
  0.0 20.2 %shard_map.55 = bf16[12,1024]{1,0:T(8,128)(2,1)S(1)} custom-call(bf16[48,256]{1,0:T(8,128)(2,1)} %q_hbm.1, bf16[1,8,128,1024]{3,2,1,0:T(8,128)(2,1)} %k_hbm.1, bf16[1,8,128,1024]{3,2,1,0:T(8,128)(2,1)} %v_hbm.1, s32[1,4]{1,0:T(1,128)} %len_hbm.1, s32[1,4,32]{2,1,0:T(4,128)} %table_hbm.1), custom_call_target="tpu_custom_call" | custom-call | tf_op jit(solution)/shard_map/pallas_call | solution.py:353
  20.2 0.6 %copy.7 = bf16[12,1024]{1,0:T(8,128)(2,1)} copy(bf16[12,1024]{1,0:T(8,128)(2,1)S(1)} %shard_map.55) | data formatting | bytes 49152
where the time goes:
time: 20.9 us; the launch traced here: 20.8 us
  Pallas kernels  20.2 us (97%)
  local copies, waits for them, and re-layouts  0.62 us (3%)
    pallas_call x1, Pallas kernels, fused_body(): pl.pallas_call(functools.partial(fused, n_blk, n_grp, seqs, tokens, heads...  20.2 us
    unnamed x1, local copies, waits for them, and re-layouts  0.62 us

commit v1 on v0

--- a/solution.py
+++ b/solution.py
@@ -155,10 +155,10 @@
     for s in range(slots):
         kv_copies.append(pltpu.make_async_copy(k_hbm.at[0, s], k_buf.at[s], kv_sem.at[0, s]))
         kv_copies.append(pltpu.make_async_copy(v_hbm.at[0, s], v_buf.at[s], kv_sem.at[1, s]))
+
+    q_copy.wait()
     for copy in kv_copies:
         copy.start()
-
-    q_copy.wait()
     q_f32[...] = q_in[...].astype(jnp.float32)
 
     def pack(group, store):

time: 20.9 us -> 20.3 us (0.971)
  Pallas kernels: 20.2 us -> 19.5 us
    pallas_call x1, Pallas kernels: 20.2 us -> 19.5 us  [fused_body(): pl.pallas_call(functools.partial(fused, n_blk, n_grp, seqs, tokens, heads...]
where the time goes in v1:
time: 20.3 us; the launch traced here: 20.1 us
  Pallas kernels  19.5 us (96%)
  local copies, waits for them, and re-layouts  0.62 us (3%)
    pallas_call x1, Pallas kernels, fused_body(): pl.pallas_call(functools.partial(fused, n_blk, n_grp, seqs, tokens, heads...  19.5 us
    unnamed x1, local copies, waits for them, and re-layouts  0.62 us

profile of v1, /device:TPU:0, one launch (start us, length us, event | category | flops | bytes accessed | tf_op | source)
XLA Modules:
  0.0 20.1 jit_solution(15303399037719803968)
XLA Ops:
  0.0 19.5 %shard_map.55 = bf16[12,1024]{1,0:T(8,128)(2,1)S(1)} custom-call(bf16[48,256]{1,0:T(8,128)(2,1)} %q_hbm.1, bf16[1,8,128,1024]{3,2,1,0:T(8,128)(2,1)} %k_hbm.1, bf16[1,8,128,1024]{3,2,1,0:T(8,128)(2,1)} %v_hbm.1, s32[1,4]{1,0:T(1,128)} %len_hbm.1, s32[1,4,32]{2,1,0:T(4,128)} %table_hbm.1), custom_call_target="tpu_custom_call" | custom-call | tf_op jit(solution)/shard_map/pallas_call | solution.py:353
  19.5 0.6 %copy.7 = bf16[12,1024]{1,0:T(8,128)(2,1)} copy(bf16[12,1024]{1,0:T(8,128)(2,1)S(1)} %shard_map.55) | data formatting | bytes 49152

commit v2 on v1

v2 whole, which is shorter than its diff:
```python
import functools
import math

import jax
import jax.numpy as jnp
from jax import lax
from jax.experimental import pallas as pl
from jax.experimental.pallas import tpu as pltpu
from jax.sharding import PartitionSpec as P

HQ = 64
KVH = 8
DH = 128
STEPS = 3


empty_max = -1e30


def owners(seq_lengths, slot_table, first_slot, slot_count):
    slot_ids = first_slot + jnp.arange(slot_count, dtype=jnp.int32)
    places = jnp.arange(slot_table.shape[1], dtype=jnp.int32)
    in_length = places[None, :] < seq_lengths[:, None]
    matches = (slot_table[:, :, None] == slot_ids[None, None, :]) & in_length[:, :, None]
    return jnp.transpose(jnp.any(matches, axis=1))


def slot_partials(query_block, key_block, value_block):
    slot_count = key_block.shape[0]
    per_group = HQ // KVH
    grouped_q = query_block.reshape(slot_count, STEPS, KVH, per_group, DH)
    grouped_q = jnp.transpose(grouped_q, (0, 2, 1, 3, 4)).reshape(
        slot_count, KVH, STEPS * per_group, DH
    )
    key_heads = key_block.reshape(slot_count, key_block.shape[1], KVH, DH)
    value_heads = value_block.reshape(slot_count, value_block.shape[1], KVH, DH)
    scores = jnp.einsum(
        "cgqd,ctgd->cgqt", grouped_q, key_heads, preferred_element_type=jnp.float32
    ) * (1.0 / math.sqrt(DH))
    block_max = jnp.max(scores, axis=3)
    weights = jnp.exp(scores - block_max[..., None]).astype(jnp.bfloat16)
    block_total = jnp.sum(weights.astype(jnp.float32), axis=3)
    block_out = jnp.einsum(
        "cgqt,ctgd->cgqd", weights, value_heads, preferred_element_type=jnp.float32
    )
    return (block_max, block_total, block_out)


def gather_sequences(owned, block_max, block_total, block_out):
    masked = jnp.where(owned[:, :, None, None], block_max[:, None], empty_max)
    seq_max = jnp.max(masked, axis=0)
    factor = jnp.where(owned[:, :, None, None], jnp.exp(block_max[:, None] - seq_max[None]), 0.0)
    seq_total = jnp.sum(factor * block_total[:, None], axis=0)
    seq_out = jnp.einsum("cqgh,cghd->qghd", factor, block_out, precision=lax.Precision.HIGHEST)
    seq_count = owned.shape[1]
    per_group = HQ // KVH
    seq_max = jnp.transpose(
        seq_max.reshape(seq_count, KVH, STEPS, per_group), (0, 2, 1, 3)
    ).reshape(seq_count * STEPS, HQ)
    seq_total = jnp.transpose(
        seq_total.reshape(seq_count, KVH, STEPS, per_group), (0, 2, 1, 3)
    ).reshape(seq_count * STEPS, HQ)
    seq_out = jnp.transpose(
        seq_out.reshape(seq_count, KVH, STEPS, per_group, DH), (0, 2, 1, 3, 4)
    ).reshape(seq_count * STEPS, HQ, DH)
    return (seq_max, seq_total, seq_out)


def block_summary(owned, query_seq, key_block, value_block):
    query_block = jnp.dot(
        owned.astype(jnp.bfloat16), query_seq, preferred_element_type=jnp.float32
    ).astype(jnp.bfloat16)
    block_max, block_total, block_out = slot_partials(query_block, key_block, value_block)
    return gather_sequences(owned, block_max, block_total, block_out)


def body(queries, key_pool, value_pool, lengths, block_table):
    grouped = lax.all_to_all(queries, "grp", split_axis=0, concat_axis=1, tiled=True)
    query_full = lax.all_gather(grouped, "blk", axis=1, tiled=True)
    token_count = query_full.shape[0]
    query_seq = query_full.reshape(token_count // STEPS, STEPS * query_full.shape[1])
    local_keys = key_pool[0]
    local_values = value_pool[0]
    slots_here = local_keys.shape[0]
    first_slot = lax.axis_index("blk") * slots_here
    owned = owners(lengths[0], block_table[0], first_slot, slots_here)
    seq_max, seq_total, seq_out = block_summary(owned, query_seq, local_keys, local_values)
    cycle_size = lax.axis_size("blk")
    heads_here = HQ // cycle_size
    arrived_max, arrived_total, arrived_out = (
        lax.all_to_all(seq_max[None], "blk", split_axis=2, concat_axis=0, tiled=True),
        lax.all_to_all(seq_total[None], "blk", split_axis=2, concat_axis=0, tiled=True),
        lax.all_to_all(seq_out[None], "blk", split_axis=2, concat_axis=0, tiled=True),
    )
    slice_max = jnp.max(arrived_max, axis=0)
    scaling = jnp.exp(arrived_max - slice_max[None])
    mine_total = jnp.sum(scaling * arrived_total, axis=0)
    mine_out = jnp.sum(scaling[..., None] * arrived_out, axis=0)
    attended = (mine_out / mine_total[..., None]).astype(jnp.bfloat16)
    return attended.reshape(mine_out.shape[0], heads_here * DH)


LANES = 128
SUB = 8


def flip(index, step):
    bit = 1
    while bit <= step:
        if step & bit:
            index = index + bit * (1 - 2 * ((index // bit) % 2))
        bit *= 2
    return index


def pieces_of(tokens, heads):
    out = []
    for block in range(tokens * heads // SUB):
        row = block * SUB
        parts = []
        while row < (block + 1) * SUB:
            head, token = divmod(row, tokens)
            count = min((block + 1) * SUB - row, tokens - token)
            parts.append((head, token, count))
            row += count
        out.append(parts)
    return out


def fused(
    n_blk, n_grp, seqs, tokens, heads, per_group,
    q_hbm, k_hbm, v_hbm, len_hbm, table_hbm, out_ref,
    q_in, q_f32, q_send, q_buf, k_buf, v_buf, o_send, o_recv, s_send, s_recv, o_rows,
    table_ref, len_ref, bias_ref, in_sem, kv_sem, z_send, z_recv, p_send, p_recv, o_ssem, o_rsem, s_ssem, s_rsem,
):
    b = lax.axis_index("blk")
    g = lax.axis_index("grp")
    slots, block = k_hbm.shape[1:3]
    rows = tokens * per_group
    period = bias_ref.shape[1]
    scale = math.log2(math.e) / math.sqrt(DH)

    q_copy = pltpu.make_async_copy(q_hbm, q_in, in_sem.at[0])
    table_copy = pltpu.make_async_copy(table_hbm, table_ref, in_sem.at[1])
    len_copy = pltpu.make_async_copy(len_hbm, len_ref, in_sem.at[2])
    q_copy.start()
    table_copy.start()
    len_copy.start()
    barrier = pltpu.get_barrier_semaphore()
    for d in range(1, n_grp):
        pl.semaphore_signal(barrier, inc=1, device_id={"grp": flip(g, d)}, device_id_type=pl.DeviceIdType.MESH)
    for r in range(1, n_blk):
        pl.semaphore_signal(barrier, inc=1, device_id={"blk": flip(b, r)}, device_id_type=pl.DeviceIdType.MESH)

    q_copy.wait()
    for k in range(KVH):
        lanes = pl.ds(k * DH, DH)
        pltpu.make_async_copy(k_hbm.at[0, :, :, lanes], k_buf.at[k], kv_sem.at[0]).start()
    for k in range(KVH):
        lanes = pl.ds(k * DH, DH)
        pltpu.make_async_copy(v_hbm.at[0, :, :, lanes], v_buf.at[k], kv_sem.at[1]).start()

    q_f32[...] = q_in[...].astype(jnp.float32)
    for group in range(n_grp):
        for i, parts in enumerate(pieces_of(tokens, heads)):
            parts = [
                q_f32[group * tokens + t0 : group * tokens + t0 + count, hh * DH : (hh + 1) * DH]
                for hh, t0, count in parts
            ]
            piece = parts[0] if len(parts) == 1 else jnp.concatenate(parts, axis=0)
            q_send[group, i] = piece.astype(jnp.bfloat16)
    q_buf[0, g] = q_send[g]

    pl.semaphore_wait(barrier, n_grp - 1 + n_blk - 1)

    def z_copy(d):
        there = flip(g, d)
        return pltpu.make_async_remote_copy(
            src_ref=q_send.at[there], dst_ref=q_buf.at[0, g],
            send_sem=z_send.at[0], recv_sem=z_recv.at[d],
            device_id={"grp": there}, device_id_type=pl.DeviceIdType.MESH,
        )

    def forward(group):
        for r in range(n_blk - 1, 0, -1):
            pltpu.make_async_remote_copy(
                src_ref=q_buf.at[0, group], dst_ref=q_buf.at[r, group],
                send_sem=p_send.at[0], recv_sem=p_recv.at[r // 2],
                device_id={"blk": flip(b, r)}, device_id_type=pl.DeviceIdType.MESH,
            ).start()

    def across(src, dst, send, recv):
        return pltpu.make_async_remote_copy(
            src_ref=src, dst_ref=dst, send_sem=send, recv_sem=recv,
            device_id={"blk": flip(b, 1)}, device_id_type=pl.DeviceIdType.MESH,
        )

    order = range(1, n_grp)
    z_copies = {d: z_copy(d) for d in order}
    for d in reversed(order):
        z_copies[d].start()
    forward(g)

    table_copy.wait()
    len_copy.wait()
    table = table_ref[0]
    seq_id = lax.broadcasted_iota(jnp.int32, table.shape, 0)
    place = lax.broadcasted_iota(jnp.int32, table.shape, 1)
    length = jnp.zeros(table.shape, jnp.int32)
    for q in range(seqs):
        length = jnp.where(seq_id == q, jnp.broadcast_to(len_ref[0:1, q : q + 1], table.shape), length)
    marked = jnp.where(place < length, table - b * slots, -1)
    row_seq = (lax.broadcasted_iota(jnp.int32, (period, LANES), 0) % tokens) // STEPS
    for s in range(slots):
        owner = jnp.max(jnp.where(marked == s, seq_id, -1), axis=1, keepdims=True)
        owner = jnp.max(owner, axis=0, keepdims=True)
        owner = jnp.broadcast_to(owner, (period, LANES))
        bias_ref[s] = jnp.where(owner == row_seq, 0.0, empty_max)

    for d in order:
        z_copies[d].wait_recv()
        forward(flip(g, d))

    for i, buf in enumerate((k_buf, v_buf)):
        pltpu.make_async_copy(buf, buf, kv_sem.at[i]).wait()

    def head_pair(r):
        ks = [flip(b, r), flip(b, r + 1)]
        queries = [
            q_buf[r + i].astype(jnp.float32).reshape(rows, DH).astype(jnp.bfloat16) for i in range(2)
        ]
        blank = jnp.zeros((rows, DH), jnp.bfloat16)
        both = jnp.concatenate(
            [
                jnp.concatenate([queries[0], blank], axis=1),
                jnp.concatenate([blank, queries[1]], axis=1),
            ],
            axis=0,
        )
        step = 2 if slots % 2 == 0 else 1
        scores = []
        for s in range(0, slots, step):
            keys = jnp.concatenate(
                [k_buf[k, s : s + step].reshape(step * block, DH) for k in ks], axis=1
            )
            out = lax.dot_general(
                both, keys, (((1,), (1,)), ((), ())), preferred_element_type=jnp.float32
            )
            scores += [out[:, i * block : (i + 1) * block] for i in range(step)]
        results = []
        for i, k in enumerate(ks):
            mine = []
            for s in range(slots):
                bias = jnp.concatenate([bias_ref[s]] * (rows // period), axis=0)
                mine.append(scores[s][i * rows : (i + 1) * rows] * scale + bias)
            top = mine[0]
            for s in range(1, slots):
                top = jnp.maximum(top, mine[s])
            top = jnp.broadcast_to(jnp.max(top, axis=1, keepdims=True), (rows, LANES))
            weights = jnp.concatenate([jnp.exp2(x - top).astype(jnp.bfloat16) for x in mine], axis=1)
            values = v_buf[k].reshape(slots * block, DH)
            values = jnp.concatenate([values, jnp.ones(values.shape, jnp.bfloat16)], axis=1)
            total = jnp.dot(weights, values, preferred_element_type=jnp.float32)
            results.append((total[:, :DH].astype(jnp.bfloat16), top, total[:, DH:]))
        return results

    def in_rows(results):
        lane = lax.broadcasted_iota(jnp.int32, (rows, LANES), 1)
        stats = jnp.zeros((rows, LANES), jnp.float32)
        for i, (_, top, total) in enumerate(results):
            stats = jnp.where(lane == i * SUB, top, stats)
            stats = jnp.where(lane == i * SUB + 1, total, stats)
        stats = jnp.concatenate([stats, jnp.zeros((LANES - rows, LANES), jnp.float32)], axis=0)
        return jnp.transpose(stats)[: 2 * SUB]

    def o_copy(r):
        return pltpu.make_async_remote_copy(
            src_ref=o_send.at[r], dst_ref=o_recv.at[r],
            send_sem=o_ssem.at[0], recv_sem=o_rsem.at[0],
            device_id={"blk": flip(b, r)}, device_id_type=pl.DeviceIdType.MESH,
        )

    def s_copy(r):
        return pltpu.make_async_remote_copy(
            src_ref=s_send.at[r], dst_ref=s_recv.at[r],
            send_sem=s_ssem.at[0], recv_sem=s_rsem.at[0],
            device_id={"blk": flip(b, r)}, device_id_type=pl.DeviceIdType.MESH,
        )

    def arrived(first):
        low = max(first, 1)
        part = q_buf.at[pl.ds(low, first + 2 - low)]
        across(part, part, p_send.at[0], p_recv.at[first // 2]).wait_recv()

    for first in (0, 2, 4, 6):
        arrived(first)
        results = head_pair(first)
        for i, (o, _, _) in enumerate(results):
            r = first + i
            if r:
                o_send[r] = o
                o_copy(r).start()
            else:
                o_recv[0] = o
        stats = in_rows(results)
        for i in range(2):
            r = first + i
            if r:
                s_send[r] = stats[i * SUB : (i + 1) * SUB]
                s_copy(r).start()
            else:
                s_recv[0] = stats[:SUB]

    others = pl.ds(1, n_blk - 1)
    across(s_recv.at[others], s_recv.at[others], s_ssem.at[0], s_rsem.at[0]).wait_recv()
    tops = s_recv[:, 0, :]
    factor = jnp.exp2(tops - jnp.max(tops, axis=0, keepdims=True))
    share = factor / jnp.sum(factor * s_recv[:, 1, :], axis=0, keepdims=True)
    share = jnp.concatenate([share, jnp.zeros((LANES - n_blk, LANES), jnp.float32)], axis=0)
    share = jnp.transpose(share)[:rows]
    across(o_recv.at[others], o_recv.at[others], o_ssem.at[0], o_rsem.at[0]).wait_recv()
    merged = jnp.zeros((rows, DH), jnp.float32)
    for r in range(n_blk):
        merged = merged + share[:, r : r + 1] * o_recv[r].astype(jnp.float32)
    o_rows[...] = merged
    for h in range(per_group):
        out_ref[:, h * DH : (h + 1) * DH] = o_rows[h * tokens : (h + 1) * tokens, :].astype(jnp.bfloat16)

    z_part = q_buf.at[0, pl.ds(1, n_grp - 1)]
    across(z_part, z_part, z_send.at[0], z_recv.at[0]).wait_send()
    across(q_buf.at[others], q_buf.at[others], p_send.at[0], p_recv.at[0]).wait_send()
    across(o_send.at[others], o_send.at[others], o_ssem.at[0], o_rsem.at[0]).wait_send()
    across(s_send.at[others], s_send.at[others], s_ssem.at[0], s_rsem.at[0]).wait_send()


def fused_body(n_blk, n_grp, queries, key_pool, value_pool, lengths, block_table):
    seqs = lengths.shape[1]
    tokens = seqs * STEPS
    heads = queries.shape[1] // DH
    per_group = HQ // KVH
    slots, block = key_pool.shape[1:3]
    rows = tokens * per_group
    blocks = tokens * heads // SUB
    dma = pltpu.SemaphoreType.DMA
    vmem = pl.BlockSpec(memory_space=pltpu.VMEM)
    hbm = pl.BlockSpec(memory_space=pltpu.HBM)
    return pl.pallas_call(
        functools.partial(fused, n_blk, n_grp, seqs, tokens, heads, per_group),
        out_shape=pltpu.VMEM((tokens, per_group * DH), jnp.bfloat16),
        in_specs=[hbm] * 5,
        out_specs=vmem,
        scratch_shapes=[
            pltpu.VMEM(queries.shape, jnp.bfloat16),
            pltpu.VMEM(queries.shape, jnp.float32),
            pltpu.VMEM((n_grp, blocks, SUB, DH), jnp.bfloat16),
            pltpu.VMEM((n_blk, n_grp, blocks, SUB, DH), jnp.bfloat16),
            pltpu.VMEM((KVH, slots, block, DH), jnp.bfloat16),
            pltpu.VMEM((KVH, slots, block, DH), jnp.bfloat16),
            pltpu.VMEM((n_blk, rows, DH), jnp.bfloat16),
            pltpu.VMEM((n_blk, rows, DH), jnp.bfloat16),
            pltpu.VMEM((n_blk, SUB, LANES), jnp.float32),
            pltpu.VMEM((n_blk, SUB, LANES), jnp.float32),
            pltpu.VMEM((rows, DH), jnp.float32),
            pltpu.VMEM(block_table.shape, jnp.int32),
            pltpu.VMEM(lengths.shape, jnp.int32),
            pltpu.VMEM((slots, math.lcm(tokens, SUB), LANES), jnp.float32),
            dma((3,)), dma((2,)),
            dma((1,)), dma((n_grp,)),
            dma((1,)), dma((n_blk // 2,)),
            dma((1,)), dma((1,)),
            dma((1,)), dma((1,)),
        ],
        compiler_params=pltpu.CompilerParams(
            collective_id=0, has_side_effects=True, vmem_limit_bytes=62914560
        ),
    )(queries, key_pool, value_pool, lengths, block_table)


def choose(mesh):
    n_blk, n_grp = mesh.shape["blk"], mesh.shape["grp"]

    def run(queries, key_pool, value_pool, lengths, block_table):
        rows = lengths.shape[1] * HQ // KVH * STEPS
        fits = (
            n_blk == KVH
            and n_blk & (n_blk - 1) == 0
            and n_grp & (n_grp - 1) == 0
            and queries.shape[1] % DH == 0
            and (lengths.shape[1] * STEPS * queries.shape[1] // DH) % SUB == 0
            and rows % math.lcm(lengths.shape[1] * STEPS, SUB) == 0
            and rows % 16 == 0
            and rows <= LANES
            and key_pool.shape[2] == LANES
        )
        if not fits:
            return body(queries, key_pool, value_pool, lengths, block_table)
        return fused_body(n_blk, n_grp, queries, key_pool, value_pool, lengths, block_table)

    return run


def solution(mesh):
    placed = (
        P(None, ("blk", "grp")),
        P("grp", "blk", None, None),
        P("grp", "blk", None, None),
        P("grp", None),
        P("grp", None, None),
    )
    return jax.shard_map(
        choose(mesh), mesh=mesh, in_specs=placed, out_specs=P("grp", "blk"), check_vma=False
    )
```

time: 20.3 us -> 18.5 us (0.911)
  Pallas kernels: 19.5 us -> 17.7 us
    pallas_call x1, Pallas kernels: 19.5 us -> 17.7 us  [fused_body(): pl.pallas_call(functools.partial(fused, n_blk, n_grp, seqs, tokens, heads...]
where the time goes in v2:
time: 18.5 us; the launch traced here: 18.4 us
  Pallas kernels  17.7 us (96%)
  local copies, waits for them, and re-layouts  0.62 us (3%)
    pallas_call x1, Pallas kernels, fused_body(): pl.pallas_call(functools.partial(fused, n_blk, n_grp, seqs, tokens, heads...  17.7 us
    unnamed x1, local copies, waits for them, and re-layouts  0.62 us

profile of v2, /device:TPU:0, one launch (start us, length us, event | category | flops | bytes accessed | tf_op | source)
XLA Modules:
  0.0 18.4 jit_solution(13806761569698312548)
XLA Ops:
  0.0 17.7 %shard_map.55 = bf16[12,1024]{1,0:T(8,128)(2,1)S(1)} custom-call(bf16[48,256]{1,0:T(8,128)(2,1)} %q_hbm.1, bf16[1,8,128,1024]{3,2,1,0:T(8,128)(2,1)} %k_hbm.1, bf16[1,8,128,1024]{3,2,1,0:T(8,128)(2,1)} %v_hbm.1, s32[1,4]{1,0:T(1,128)} %len_hbm.1, s32[1,4,32]{2,1,0:T(4,128)} %table_hbm.1), custom_call_target="tpu_custom_call" | custom-call | tf_op jit(solution)/shard_map/pallas_call | solution.py:347
  17.8 0.6 %copy.7 = bf16[12,1024]{1,0:T(8,128)(2,1)} copy(bf16[12,1024]{1,0:T(8,128)(2,1)S(1)} %shard_map.55) | data formatting | bytes 49152

commit v3 on v2

--- a/solution.py
+++ b/solution.py
@@ -131,7 +131,7 @@
     n_blk, n_grp, seqs, tokens, heads, per_group,
     q_hbm, k_hbm, v_hbm, len_hbm, table_hbm, out_ref,
     q_in, q_f32, q_send, q_buf, k_buf, v_buf, o_send, o_recv, s_send, s_recv, o_rows,
-    table_ref, len_ref, bias_ref, in_sem, kv_sem, z_send, z_recv, p_send, p_recv, o_ssem, o_rsem, s_ssem, s_rsem,
+    table_ref, len_ref, bias_ref, in_sem, kv_sem, z_send, z_recv, p_send, p_recv, d_send, o_ssem, o_rsem, s_ssem, s_rsem, ready,
 ):
     b = lax.axis_index("blk")
     g = lax.axis_index("grp")
@@ -147,10 +147,20 @@
     table_copy.start()
     len_copy.start()
     barrier = pltpu.get_barrier_semaphore()
+    side, up = n_blk // 4, n_blk // 2
+    near = [r for r in range(1, n_blk) if not (r & side and r & up)]
     for d in range(1, n_grp):
         pl.semaphore_signal(barrier, inc=1, device_id={"grp": flip(g, d)}, device_id_type=pl.DeviceIdType.MESH)
-    for r in range(1, n_blk):
+    for r in near:
         pl.semaphore_signal(barrier, inc=1, device_id={"blk": flip(b, r)}, device_id_type=pl.DeviceIdType.MESH)
+
+    @pl.when(g == 0)
+    def _():
+        for r in range(1, n_blk):
+            pl.semaphore_signal(
+                barrier, inc=1, device_id={"blk": flip(b, r), "grp": n_grp - 1},
+                device_id_type=pl.DeviceIdType.MESH,
+            )
 
     q_copy.wait()
     for k in range(KVH):
@@ -171,7 +181,7 @@
             q_send[group, i] = piece.astype(jnp.bfloat16)
     q_buf[0, g] = q_send[g]
 
-    pl.semaphore_wait(barrier, n_grp - 1 + n_blk - 1)
+    pl.semaphore_wait(barrier, n_grp - 1 + len(near) + g // (n_grp - 1) * (n_blk - 1))
 
     def z_copy(d):
         there = flip(g, d)
@@ -181,11 +191,11 @@
             device_id={"grp": there}, device_id_type=pl.DeviceIdType.MESH,
         )
 
-    def forward(group):
-        for r in range(n_blk - 1, 0, -1):
+    def forward(group, targets=tuple(range(n_blk - 1, 0, -1))):
+        for r in targets:
             pltpu.make_async_remote_copy(
                 src_ref=q_buf.at[0, group], dst_ref=q_buf.at[r, group],
-                send_sem=p_send.at[0], recv_sem=p_recv.at[r // 2],
+                send_sem=p_send.at[0], recv_sem=p_recv.at[r],
                 device_id={"blk": flip(b, r)}, device_id_type=pl.DeviceIdType.MESH,
             ).start()
 
@@ -197,9 +207,25 @@
 
     order = range(1, n_grp)
     z_copies = {d: z_copy(d) for d in order}
-    for d in reversed(order):
+    far = n_grp - 1
+    for d in reversed(order[:-1]):
         z_copies[d].start()
-    forward(g)
+
+    @pl.when(g == far)
+    def _():
+        for r in reversed(range(n_blk)):
+            pltpu.make_async_remote_copy(
+                src_ref=q_send.at[0], dst_ref=q_buf.at[r, g],
+                send_sem=d_send.at[0], recv_sem=p_recv.at[r] if r else z_recv.at[far],
+                device_id={"blk": flip(b, r), "grp": 0}, device_id_type=pl.DeviceIdType.MESH,
+            ).start()
+
+    @pl.when(g != far)
+    def _():
+        z_copies[far].start()
+
+    pl.semaphore_signal(ready, inc=1, device_id={"blk": flip(b, side)}, device_id_type=pl.DeviceIdType.MESH)
+    forward(g, near)
 
     table_copy.wait()
     len_copy.wait()
@@ -217,17 +243,24 @@
         owner = jnp.broadcast_to(owner, (period, LANES))
         bias_ref[s] = jnp.where(owner == row_seq, 0.0, empty_max)
 
+    pl.semaphore_wait(ready, 1)
+    forward(g, [r for r in range(1, n_blk) if r not in near])
     for d in order:
         z_copies[d].wait_recv()
-        forward(flip(g, d))
+        if d < far:
+            forward(flip(g, d))
+
+    @pl.when(g > 0)
+    def _():
+        forward(flip(g, far))
 
     for i, buf in enumerate((k_buf, v_buf)):
         pltpu.make_async_copy(buf, buf, kv_sem.at[i]).wait()
 
-    def head_pair(r):
-        ks = [flip(b, r), flip(b, r + 1)]
+    def head_pair(pair):
+        ks = [flip(b, r) for r in pair]
         queries = [
-            q_buf[r + i].astype(jnp.float32).reshape(rows, DH).astype(jnp.bfloat16) for i in range(2)
+            q_buf[r].astype(jnp.float32).reshape(rows, DH).astype(jnp.bfloat16) for r in pair
         ]
         blank = jnp.zeros((rows, DH), jnp.bfloat16)
         both = jnp.concatenate(
@@ -287,29 +320,27 @@
             device_id={"blk": flip(b, r)}, device_id_type=pl.DeviceIdType.MESH,
         )
 
-    def arrived(first):
-        low = max(first, 1)
-        part = q_buf.at[pl.ds(low, first + 2 - low)]
-        across(part, part, p_send.at[0], p_recv.at[first // 2]).wait_recv()
-
-    for first in (0, 2, 4, 6):
-        arrived(first)
-        results = head_pair(first)
-        for i, (o, _, _) in enumerate(results):
-            r = first + i
+    def arrived(pair):
+        for r in pair:
+            if r:
+                across(q_buf.at[r], q_buf.at[r], p_send.at[0], p_recv.at[r]).wait_recv()
+
+    for pair in ((0,1),(2,4),(6,7),(3,5)):
+        arrived(pair)
+        results = head_pair(pair)
+        for r, (o, _, _) in zip(pair, results):
             if r:
                 o_send[r] = o
                 o_copy(r).start()
             else:
                 o_recv[0] = o
         stats = in_rows(results)
-        for i in range(2):
-            r = first + i
+        for i, r in enumerate(pair):
             if r:
-                s_send[r] = stats[i * SUB : (i + 1) * SUB]
+                s_send[r] = stats[i * SUB : i * SUB + 2]
                 s_copy(r).start()
             else:
-                s_recv[0] = stats[:SUB]
+                s_recv[0] = stats[:2]
 
     others = pl.ds(1, n_blk - 1)
     across(s_recv.at[others], s_recv.at[others], s_ssem.at[0], s_rsem.at[0]).wait_recv()
@@ -326,9 +357,26 @@
     for h in range(per_group):
         out_ref[:, h * DH : (h + 1) * DH] = o_rows[h * tokens : (h + 1) * tokens, :].astype(jnp.bfloat16)
 
-    z_part = q_buf.at[0, pl.ds(1, n_grp - 1)]
-    across(z_part, z_part, z_send.at[0], z_recv.at[0]).wait_send()
-    across(q_buf.at[others], q_buf.at[others], p_send.at[0], p_recv.at[0]).wait_send()
+    def sent(part, sem):
+        across(part, part, sem, p_recv.at[0]).wait_send()
+
+    @pl.when(g == far)
+    def _():
+        sent(q_buf.at[0, pl.ds(1, n_grp - 2)], z_send.at[0])
+        sent(q_buf.at[:, 0], d_send.at[0])
+
+    @pl.when(g != far)
+    def _():
+        sent(q_buf.at[0, pl.ds(1, n_grp - 1)], z_send.at[0])
+
+    @pl.when(g == 0)
+    def _():
+        sent(q_buf.at[others, pl.ds(1, n_grp - 1)], p_send.at[0])
+
+    @pl.when(g > 0)
+    def _():
+        sent(q_buf.at[others], p_send.at[0])
+
     across(o_send.at[others], o_send.at[others], o_ssem.at[0], o_rsem.at[0]).wait_send()
     across(s_send.at[others], s_send.at[others], s_ssem.at[0], s_rsem.at[0]).wait_send()
 
@@ -358,17 +406,17 @@
             pltpu.VMEM((KVH, slots, block, DH), jnp.bfloat16),
             pltpu.VMEM((n_blk, rows, DH), jnp.bfloat16),
             pltpu.VMEM((n_blk, rows, DH), jnp.bfloat16),
-            pltpu.VMEM((n_blk, SUB, LANES), jnp.float32),
-            pltpu.VMEM((n_blk, SUB, LANES), jnp.float32),
+            pltpu.VMEM((n_blk, 2, LANES), jnp.float32),
+            pltpu.VMEM((n_blk, 2, LANES), jnp.float32),
             pltpu.VMEM((rows, DH), jnp.float32),
             pltpu.VMEM(block_table.shape, jnp.int32),
             pltpu.VMEM(lengths.shape, jnp.int32),
             pltpu.VMEM((slots, math.lcm(tokens, SUB), LANES), jnp.float32),
             dma((3,)), dma((2,)),
             dma((1,)), dma((n_grp,)),
-            dma((1,)), dma((n_blk // 2,)),
+            dma((1,)), dma((n_blk,)), dma((1,)),
             dma((1,)), dma((1,)),
-            dma((1,)), dma((1,)),
+            dma((1,)), dma((1,)), pltpu.SemaphoreType.REGULAR,
         ],
         compiler_params=pltpu.CompilerParams(
             collective_id=0, has_side_effects=True, vmem_limit_bytes=62914560

time: 18.5 us -> 17.1 us (0.924)
  Pallas kernels: 17.7 us -> 16.3 us
    pallas_call x1, Pallas kernels: 17.7 us -> 16.3 us  [fused_body(): pl.pallas_call(functools.partial(fused, n_blk, n_grp, seqs, tokens, heads...]
where the time goes in v3:
time: 17.1 us; the launch traced here: 17 us
  Pallas kernels  16.3 us (95%)
  local copies, waits for them, and re-layouts  0.62 us (4%)
    pallas_call x1, Pallas kernels, fused_body(): pl.pallas_call(functools.partial(fused, n_blk, n_grp, seqs, tokens, heads...  16.3 us
    unnamed x1, local copies, waits for them, and re-layouts  0.62 us

profile of v3, /device:TPU:0, one launch (start us, length us, event | category | flops | bytes accessed | tf_op | source)
XLA Modules:
  0.0 17.0 jit_solution(4448425639245371258)
XLA Ops:
  0.0 16.3 %shard_map.55 = bf16[12,1024]{1,0:T(8,128)(2,1)S(1)} custom-call(bf16[48,256]{1,0:T(8,128)(2,1)} %q_hbm.1, bf16[1,8,128,1024]{3,2,1,0:T(8,128)(2,1)} %k_hbm.1, bf16[1,8,128,1024]{3,2,1,0:T(8,128)(2,1)} %v_hbm.1, s32[1,4]{1,0:T(1,128)} %len_hbm.1, s32[1,4,32]{2,1,0:T(4,128)} %table_hbm.1), custom_call_target="tpu_custom_call" | custom-call | tf_op jit(solution)/shard_map/pallas_call | solution.py:395
  16.3 0.6 %copy.7 = bf16[12,1024]{1,0:T(8,128)(2,1)} copy(bf16[12,1024]{1,0:T(8,128)(2,1)S(1)} %shard_map.55) | data formatting | bytes 49152

commit v4 on v2

--- a/solution.py
+++ b/solution.py
@@ -130,8 +130,9 @@
 def fused(
     n_blk, n_grp, seqs, tokens, heads, per_group,
     q_hbm, k_hbm, v_hbm, len_hbm, table_hbm, out_ref,
-    q_in, q_f32, q_send, q_buf, k_buf, v_buf, o_send, o_recv, s_send, s_recv, o_rows,
-    table_ref, len_ref, bias_ref, in_sem, kv_sem, z_send, z_recv, p_send, p_recv, o_ssem, o_rsem, s_ssem, s_rsem,
+    q_in, q_f32, q_send, q_own, q_buf, k_buf, v_buf, o_send, o_recv, s_send, s_recv, o_rows,
+    table_ref, len_ref, bias_ref, in_sem, kv_sem, kv_send, kv_recv,
+    z_send, z_recv, p_send, p_recv, d_send, o_ssem, o_rsem, s_ssem, s_rsem,
 ):
     b = lax.axis_index("blk")
     g = lax.axis_index("grp")
@@ -139,6 +140,23 @@
     rows = tokens * per_group
     period = bias_ref.shape[1]
     scale = math.log2(math.e) / math.sqrt(DH)
+    core = b % 2
+    units = n_blk // 2
+    peers = [2 * x + 1 for x in range(units)]
+    direct = [d for d in (3,) if d < n_grp]
+    here = pl.ds(core * slots, slots)
+
+    def signal(device):
+        pl.semaphore_signal(barrier, inc=1, device_id=device, device_id_type=pl.DeviceIdType.MESH)
+
+    def remote(src, dst, send, recv, device):
+        return pltpu.make_async_remote_copy(
+            src_ref=src, dst_ref=dst, send_sem=send, recv_sem=recv,
+            device_id=device, device_id_type=pl.DeviceIdType.MESH,
+        )
+
+    def like(part, send, recv):
+        return remote(part, part, send, recv, {"blk": flip(b, 1)})
 
     q_copy = pltpu.make_async_copy(q_hbm, q_in, in_sem.at[0])
     table_copy = pltpu.make_async_copy(table_hbm, table_ref, in_sem.at[1])
@@ -147,18 +165,28 @@
     table_copy.start()
     len_copy.start()
     barrier = pltpu.get_barrier_semaphore()
+    plane = sorted({1, *peers} - {0})
+    cross = [r for r in peers if r]
     for d in range(1, n_grp):
-        pl.semaphore_signal(barrier, inc=1, device_id={"grp": flip(g, d)}, device_id_type=pl.DeviceIdType.MESH)
-    for r in range(1, n_blk):
-        pl.semaphore_signal(barrier, inc=1, device_id={"blk": flip(b, r)}, device_id_type=pl.DeviceIdType.MESH)
+        signal({"grp": flip(g, d)})
+    for r in plane:
+        signal({"blk": flip(b, r)})
+
+    @pl.when(g == 0)
+    def _():
+        for d in direct:
+            for r in cross:
+                signal({"blk": flip(b, r), "grp": d})
 
     q_copy.wait()
-    for k in range(KVH):
-        lanes = pl.ds(k * DH, DH)
-        pltpu.make_async_copy(k_hbm.at[0, :, :, lanes], k_buf.at[k], kv_sem.at[0]).start()
-    for k in range(KVH):
-        lanes = pl.ds(k * DH, DH)
-        pltpu.make_async_copy(v_hbm.at[0, :, :, lanes], v_buf.at[k], kv_sem.at[1]).start()
+    sources = ((k_hbm, k_buf), (v_hbm, v_buf))
+
+    def lanes(r):
+        return pl.ds(pl.multiple_of(flip(b, r) * DH, DH), DH)
+
+    for i, (src, dst) in enumerate(sources):
+        for x, r in enumerate(peers):
+            pltpu.make_async_copy(src.at[0, :, :, lanes(r)], dst.at[x, here], kv_sem.at[i]).start()
 
     q_f32[...] = q_in[...].astype(jnp.float32)
     for group in range(n_grp):
@@ -169,37 +197,48 @@
             ]
             piece = parts[0] if len(parts) == 1 else jnp.concatenate(parts, axis=0)
             q_send[group, i] = piece.astype(jnp.bfloat16)
-    q_buf[0, g] = q_send[g]
-
-    pl.semaphore_wait(barrier, n_grp - 1 + n_blk - 1)
+    q_own[g] = q_send[g]
+
+    crossed = 0
+    for d in direct:
+        crossed = crossed + (1 - jnp.minimum(jnp.abs(g - d), 1)) * len(cross)
+    pl.semaphore_wait(barrier, n_grp - 1 + len(plane) + crossed)
+
+    order = range(1, n_grp)
 
     def z_copy(d):
         there = flip(g, d)
-        return pltpu.make_async_remote_copy(
-            src_ref=q_send.at[there], dst_ref=q_buf.at[0, g],
-            send_sem=z_send.at[0], recv_sem=z_recv.at[d],
-            device_id={"grp": there}, device_id_type=pl.DeviceIdType.MESH,
-        )
+        return remote(q_send.at[there], q_own.at[g], z_send.at[d], z_recv.at[d], {"grp": there})
 
     def forward(group):
-        for r in range(n_blk - 1, 0, -1):
-            pltpu.make_async_remote_copy(
-                src_ref=q_buf.at[0, group], dst_ref=q_buf.at[r, group],
-                send_sem=p_send.at[0], recv_sem=p_recv.at[r // 2],
-                device_id={"blk": flip(b, r)}, device_id_type=pl.DeviceIdType.MESH,
+        for r in reversed(peers):
+            if r:
+                remote(
+                    q_own.at[group], q_buf.at[r // 2, group], p_send.at[0], p_recv.at[r // 2],
+                    {"blk": flip(b, r)},
+                ).start()
+
+    for d in reversed(order):
+        if d in direct:
+            pl.when(g != d)(z_copy(d).start)
+        else:
+            z_copy(d).start()
+    for d in direct:
+        @pl.when(g == d)
+        def _(d=d):
+            for r in reversed(cross):
+                remote(
+                    q_send.at[0], q_buf.at[r // 2, g], d_send.at[0], p_recv.at[r // 2],
+                    {"blk": flip(b, r), "grp": 0},
+                ).start()
+    forward(g)
+
+    for i, (src, dst) in enumerate(sources):
+        for x, r in enumerate(peers):
+            remote(
+                src.at[0, :, :, lanes(r - 1)], dst.at[x, here], kv_send.at[i], kv_recv.at[i],
+                {"blk": flip(b, 1)},
             ).start()
-
-    def across(src, dst, send, recv):
-        return pltpu.make_async_remote_copy(
-            src_ref=src, dst_ref=dst, send_sem=send, recv_sem=recv,
-            device_id={"blk": flip(b, 1)}, device_id_type=pl.DeviceIdType.MESH,
-        )
-
-    order = range(1, n_grp)
-    z_copies = {d: z_copy(d) for d in order}
-    for d in reversed(order):
-        z_copies[d].start()
-    forward(g)
 
     table_copy.wait()
     len_copy.wait()
@@ -209,128 +248,127 @@
     length = jnp.zeros(table.shape, jnp.int32)
     for q in range(seqs):
         length = jnp.where(seq_id == q, jnp.broadcast_to(len_ref[0:1, q : q + 1], table.shape), length)
-    marked = jnp.where(place < length, table - b * slots, -1)
+    marked = jnp.where(place < length, table - b // 2 * 2 * slots, -1)
     row_seq = (lax.broadcasted_iota(jnp.int32, (period, LANES), 0) % tokens) // STEPS
-    for s in range(slots):
+    for s in range(2 * slots):
         owner = jnp.max(jnp.where(marked == s, seq_id, -1), axis=1, keepdims=True)
         owner = jnp.max(owner, axis=0, keepdims=True)
         owner = jnp.broadcast_to(owner, (period, LANES))
         bias_ref[s] = jnp.where(owner == row_seq, 0.0, empty_max)
 
+    def take(d):
+        z_copy(d).wait_recv()
+        forward(flip(g, d))
+
     for d in order:
-        z_copies[d].wait_recv()
-        forward(flip(g, d))
-
-    for i, buf in enumerate((k_buf, v_buf)):
-        pltpu.make_async_copy(buf, buf, kv_sem.at[i]).wait()
-
-    def head_pair(r):
-        ks = [flip(b, r), flip(b, r + 1)]
-        queries = [
-            q_buf[r + i].astype(jnp.float32).reshape(rows, DH).astype(jnp.bfloat16) for i in range(2)
-        ]
+        if d in direct:
+            pl.when(g > 0)(functools.partial(take, d))
+        else:
+            take(d)
+
+    for i, (_, buf) in enumerate(sources):
+        pltpu.make_async_copy(buf.at[:, here], buf.at[:, here], kv_sem.at[i]).wait()
+
+    def unit(x):
+        query = q_buf[x].astype(jnp.float32).reshape(rows, DH).astype(jnp.bfloat16)
         blank = jnp.zeros((rows, DH), jnp.bfloat16)
         both = jnp.concatenate(
-            [
-                jnp.concatenate([queries[0], blank], axis=1),
-                jnp.concatenate([blank, queries[1]], axis=1),
-            ],
-            axis=0,
+            [jnp.concatenate([query, blank], axis=1), jnp.concatenate([blank, query], axis=1)], axis=0
         )
         step = 2 if slots % 2 == 0 else 1
         scores = []
         for s in range(0, slots, step):
             keys = jnp.concatenate(
-                [k_buf[k, s : s + step].reshape(step * block, DH) for k in ks], axis=1
+                [k_buf[x, half * slots + s : half * slots + s + step].reshape(step * block, DH) for half in range(2)],
+                axis=1,
             )
             out = lax.dot_general(
                 both, keys, (((1,), (1,)), ((), ())), preferred_element_type=jnp.float32
             )
             scores += [out[:, i * block : (i + 1) * block] for i in range(step)]
-        results = []
-        for i, k in enumerate(ks):
+        tops, totals = [], []
+        for half in range(2):
             mine = []
             for s in range(slots):
-                bias = jnp.concatenate([bias_ref[s]] * (rows // period), axis=0)
-                mine.append(scores[s][i * rows : (i + 1) * rows] * scale + bias)
+                bias = jnp.concatenate([bias_ref[half * slots + s]] * (rows // period), axis=0)
+                mine.append(scores[s][half * rows : (half + 1) * rows] * scale + bias)
             top = mine[0]
-            for s in range(1, slots):
-                top = jnp.maximum(top, mine[s])
+            for score in mine[1:]:
+                top = jnp.maximum(top, score)
             top = jnp.broadcast_to(jnp.max(top, axis=1, keepdims=True), (rows, LANES))
-            weights = jnp.concatenate([jnp.exp2(x - top).astype(jnp.bfloat16) for x in mine], axis=1)
-            values = v_buf[k].reshape(slots * block, DH)
+            weights = jnp.concatenate([jnp.exp2(score - top).astype(jnp.bfloat16) for score in mine], axis=1)
+            values = v_buf[x, half * slots : (half + 1) * slots].reshape(slots * block, DH)
             values = jnp.concatenate([values, jnp.ones(values.shape, jnp.bfloat16)], axis=1)
-            total = jnp.dot(weights, values, preferred_element_type=jnp.float32)
-            results.append((total[:, :DH].astype(jnp.bfloat16), top, total[:, DH:]))
-        return results
-
-    def in_rows(results):
+            totals.append(jnp.dot(weights, values, preferred_element_type=jnp.float32))
+            tops.append(top)
+        top = jnp.maximum(tops[0], tops[1])
+        parts = [jnp.exp2(t - top) for t in tops]
+        o = totals[0][:, :DH] * parts[0] + totals[1][:, :DH] * parts[1]
+        total = totals[0][:, DH:] * parts[0] + totals[1][:, DH:] * parts[1]
+        return o.astype(jnp.bfloat16), top, total
+
+    def in_rows(top, total):
         lane = lax.broadcasted_iota(jnp.int32, (rows, LANES), 1)
-        stats = jnp.zeros((rows, LANES), jnp.float32)
-        for i, (_, top, total) in enumerate(results):
-            stats = jnp.where(lane == i * SUB, top, stats)
-            stats = jnp.where(lane == i * SUB + 1, total, stats)
+        stats = jnp.where(lane == 0, top, total)
         stats = jnp.concatenate([stats, jnp.zeros((LANES - rows, LANES), jnp.float32)], axis=0)
-        return jnp.transpose(stats)[: 2 * SUB]
-
-    def o_copy(r):
-        return pltpu.make_async_remote_copy(
-            src_ref=o_send.at[r], dst_ref=o_recv.at[r],
-            send_sem=o_ssem.at[0], recv_sem=o_rsem.at[0],
-            device_id={"blk": flip(b, r)}, device_id_type=pl.DeviceIdType.MESH,
-        )
-
-    def s_copy(r):
-        return pltpu.make_async_remote_copy(
-            src_ref=s_send.at[r], dst_ref=s_recv.at[r],
-            send_sem=s_ssem.at[0], recv_sem=s_rsem.at[0],
-            device_id={"blk": flip(b, r)}, device_id_type=pl.DeviceIdType.MESH,
-        )
-
-    def arrived(first):
-        low = max(first, 1)
-        part = q_buf.at[pl.ds(low, first + 2 - low)]
-        across(part, part, p_send.at[0], p_recv.at[first // 2]).wait_recv()
-
-    for first in (0, 2, 4, 6):
-        arrived(first)
-        results = head_pair(first)
-        for i, (o, _, _) in enumerate(results):
-            r = first + i
-            if r:
-                o_send[r] = o
-                o_copy(r).start()
-            else:
-                o_recv[0] = o
-        stats = in_rows(results)
-        for i in range(2):
-            r = first + i
-            if r:
-                s_send[r] = stats[i * SUB : (i + 1) * SUB]
-                s_copy(r).start()
-            else:
-                s_recv[0] = stats[:SUB]
-
-    others = pl.ds(1, n_blk - 1)
-    across(s_recv.at[others], s_recv.at[others], s_ssem.at[0], s_rsem.at[0]).wait_recv()
+        return jnp.transpose(stats)[:2]
+
+    for i, (_, buf) in enumerate(sources):
+        like(buf.at[:, here], kv_send.at[i], kv_recv.at[i]).wait_recv()
+
+    for x in (0, 3, 1, 2):
+        r = peers[x]
+        if r:
+            part = q_buf.at[x]
+            like(part, p_send.at[0], p_recv.at[x]).wait_recv()
+        o, top, total = unit(x)
+        if r:
+            o_send[x] = o
+            remote(o_send.at[x], o_recv.at[x], o_ssem.at[0], o_rsem.at[0], {"blk": flip(b, r)}).start()
+            s_send[x] = in_rows(top, total)
+            remote(s_send.at[x], s_recv.at[x], s_ssem.at[0], s_rsem.at[0], {"blk": flip(b, r)}).start()
+        else:
+            o_recv[x] = o
+            s_recv[x] = in_rows(top, total)
+
+    others = pl.ds(0, units)
+    like(s_recv.at[others], s_ssem.at[0], s_rsem.at[0]).wait_recv()
     tops = s_recv[:, 0, :]
     factor = jnp.exp2(tops - jnp.max(tops, axis=0, keepdims=True))
     share = factor / jnp.sum(factor * s_recv[:, 1, :], axis=0, keepdims=True)
-    share = jnp.concatenate([share, jnp.zeros((LANES - n_blk, LANES), jnp.float32)], axis=0)
+    share = jnp.concatenate([share, jnp.zeros((LANES - units, LANES), jnp.float32)], axis=0)
     share = jnp.transpose(share)[:rows]
-    across(o_recv.at[others], o_recv.at[others], o_ssem.at[0], o_rsem.at[0]).wait_recv()
+    like(o_recv.at[others], o_ssem.at[0], o_rsem.at[0]).wait_recv()
     merged = jnp.zeros((rows, DH), jnp.float32)
-    for r in range(n_blk):
-        merged = merged + share[:, r : r + 1] * o_recv[r].astype(jnp.float32)
+    for x in range(units):
+        merged = merged + share[:, x : x + 1] * o_recv[x].astype(jnp.float32)
     o_rows[...] = merged
     for h in range(per_group):
         out_ref[:, h * DH : (h + 1) * DH] = o_rows[h * tokens : (h + 1) * tokens, :].astype(jnp.bfloat16)
 
-    z_part = q_buf.at[0, pl.ds(1, n_grp - 1)]
-    across(z_part, z_part, z_send.at[0], z_recv.at[0]).wait_send()
-    across(q_buf.at[others], q_buf.at[others], p_send.at[0], p_recv.at[0]).wait_send()
-    across(o_send.at[others], o_send.at[others], o_ssem.at[0], o_rsem.at[0]).wait_send()
-    across(s_send.at[others], s_send.at[others], s_ssem.at[0], s_rsem.at[0]).wait_send()
+    for d in order:
+        if d in direct:
+            pl.when(g != d)(z_copy(d).wait_send)
+        else:
+            z_copy(d).wait_send()
+    for d in direct:
+        @pl.when(g == d)
+        def _():
+            like(q_buf.at[pl.ds(0, len(cross)), 0], d_send.at[0], p_recv.at[0]).wait_send()
+
+    @pl.when(g == 0)
+    def _():
+        part = q_buf.at[pl.ds(0, len(cross)), pl.ds(0, n_grp - len(direct))]
+        like(part, p_send.at[0], p_recv.at[0]).wait_send()
+
+    @pl.when(g > 0)
+    def _():
+        like(q_buf.at[pl.ds(0, len(cross))], p_send.at[0], p_recv.at[0]).wait_send()
+
+    for i, (_, buf) in enumerate(sources):
+        like(buf.at[:, here], kv_send.at[i], kv_recv.at[i]).wait_send()
+    like(o_send.at[others], o_ssem.at[0], o_rsem.at[0]).wait_send()
+    like(s_send.at[others], s_ssem.at[0], s_rsem.at[0]).wait_send()
 
 
 def fused_body(n_blk, n_grp, queries, key_pool, value_pool, lengths, block_table):
@@ -341,6 +379,7 @@
     slots, block = key_pool.shape[1:3]
     rows = tokens * per_group
     blocks = tokens * heads // SUB
+    units = n_blk // 2
     dma = pltpu.SemaphoreType.DMA
     vmem = pl.BlockSpec(memory_space=pltpu.VMEM)
     hbm = pl.BlockSpec(memory_space=pltpu.HBM)
@@ -353,22 +392,22 @@
             pltpu.VMEM(queries.shape, jnp.bfloat16),
             pltpu.VMEM(queries.shape, jnp.float32),
             pltpu.VMEM((n_grp, blocks, SUB, DH), jnp.bfloat16),
-            pltpu.VMEM((n_blk, n_grp, blocks, SUB, DH), jnp.bfloat16),
-            pltpu.VMEM((KVH, slots, block, DH), jnp.bfloat16),
-            pltpu.VMEM((KVH, slots, block, DH), jnp.bfloat16),
-            pltpu.VMEM((n_blk, rows, DH), jnp.bfloat16),
-            pltpu.VMEM((n_blk, rows, DH), jnp.bfloat16),
-            pltpu.VMEM((n_blk, SUB, LANES), jnp.float32),
-            pltpu.VMEM((n_blk, SUB, LANES), jnp.float32),
+            pltpu.VMEM((n_grp, blocks, SUB, DH), jnp.bfloat16),
+            pltpu.VMEM((units, n_grp, blocks, SUB, DH), jnp.bfloat16),
+            pltpu.VMEM((units, 2 * slots, block, DH), jnp.bfloat16),
+            pltpu.VMEM((units, 2 * slots, block, DH), jnp.bfloat16),
+            pltpu.VMEM((units, rows, DH), jnp.bfloat16),
+            pltpu.VMEM((units, rows, DH), jnp.bfloat16),
+            pltpu.VMEM((units, 2, LANES), jnp.float32),
+            pltpu.VMEM((units, 2, LANES), jnp.float32),
             pltpu.VMEM((rows, DH), jnp.float32),
             pltpu.VMEM(block_table.shape, jnp.int32),
             pltpu.VMEM(lengths.shape, jnp.int32),
-            pltpu.VMEM((slots, math.lcm(tokens, SUB), LANES), jnp.float32),
-            dma((3,)), dma((2,)),
-            dma((1,)), dma((n_grp,)),
-            dma((1,)), dma((n_blk // 2,)),
-            dma((1,)), dma((1,)),
-            dma((1,)), dma((1,)),
+            pltpu.VMEM((2 * slots, math.lcm(tokens, SUB), LANES), jnp.float32),
+            dma((3,)), dma((2,)), dma((2,)), dma((2,)),
+            dma((n_grp,)), dma((n_grp,)),
+            dma((1,)), dma((units,)), dma((1,)),
+            dma((1,)), dma((1,)), dma((1,)), dma((1,)),
         ],
         compiler_params=pltpu.CompilerParams(
             collective_id=0, has_side_effects=True, vmem_limit_bytes=62914560

time: 18.5 us -> 16.3 us (0.88)
  Pallas kernels: 17.7 us -> 15.5 us
    pallas_call x1, Pallas kernels: 17.7 us -> 15.5 us  [fused_body(): pl.pallas_call(functools.partial(fused, n_blk, n_grp, seqs, tokens, heads...]
where the time goes in v4:
time: 16.3 us; the launch traced here: 16.1 us
  Pallas kernels  15.5 us (95%)
  local copies, waits for them, and re-layouts  0.62 us (4%)
    pallas_call x1, Pallas kernels, fused_body(): pl.pallas_call(functools.partial(fused, n_blk, n_grp, seqs, tokens, heads...  15.5 us
    unnamed x1, local copies, waits for them, and re-layouts  0.62 us

profile of v4, /device:TPU:0, one launch (start us, length us, event | category | flops | bytes accessed | tf_op | source)
XLA Modules:
  0.0 16.1 jit_solution(4932440435911451097)
XLA Ops:
  0.0 15.5 %shard_map.55 = bf16[12,1024]{1,0:T(8,128)(2,1)S(1)} custom-call(bf16[48,256]{1,0:T(8,128)(2,1)} %q_hbm.1, bf16[1,8,128,1024]{3,2,1,0:T(8,128)(2,1)} %k_hbm.1, bf16[1,8,128,1024]{3,2,1,0:T(8,128)(2,1)} %v_hbm.1, s32[1,4]{1,0:T(1,128)} %len_hbm.1, s32[1,4,32]{2,1,0:T(4,128)} %table_hbm.1), custom_call_target="tpu_custom_call" | custom-call | tf_op jit(solution)/shard_map/pallas_call | solution.py:386
  15.5 0.6 %copy.7 = bf16[12,1024]{1,0:T(8,128)(2,1)} copy(bf16[12,1024]{1,0:T(8,128)(2,1)S(1)} %shard_map.55) | data formatting | bytes 49152
